TPU v7x, 512 devices: a whole 4x8x8 slice. The times are simulated.
512 devices in a mesh: row: 32 (over z, x_hi, core), col: 16 (over y, x_lo).
Axes of the slice: x: 4 (x_hi: 2, x_lo: 2; x = x_hi * 2 + x_lo), y: 8, z: 8, core: 2. Of those that a mesh axis runs over, the one named last changes fastest.
Arguments:
- ancestor: float32 [32, 384, 12288], P(None, 'col', 'row'), may hold values from -6 to 6
- panels: float32 [2, 12288, 512], P(None, ('row', 'col')), may hold values from -0.06 to 0.06
- link_panels: float32 [1, 512, 512], P(None, 'row'), may hold values from -0.25 to 0.25
- diag_inverse: float32 [2, 512, 512], P(None, 'row'), may hold values from -0.25 to 0.25
- blocks: int32 [2, 48], replicated, may hold values from 0 to 95, as said below
Outputs:
- columns: float32 [2, 12288, 512], P(None, ('row', 'col'))
- diagonal: float32 [2, 512, 512], P(None, 'row', 'col')
Inputs may be any that keep to these rules, and one draw needn't show every extreme that they name: Each of the 2 rows names 48 different row blocks.
All inputs are finite; a program needn't handle non-finite values.
Results may differ from a plain program's by a relative error of at most 0.0001.
Values sent between devices are 32-bit elements; how exact they have to be, the bound alone decides.
A program may use at most 64 MiB of HBM per device.

v0:
```python
import jax
import jax.numpy as jnp
from jax import lax
from jax.sharding import Mesh
from jax.sharding import PartitionSpec as P

BLOCK = 128
ROW = ("row_0", "row_1", "row_2")
ROW_COL = ("row_0", "row_1", "row_2", "col")


def joined_along(blocks, dim):
    blocks = jnp.moveaxis(blocks, 0, dim)
    shape = blocks.shape
    return blocks.reshape(*shape[:dim], shape[dim] * shape[dim + 1], *shape[dim + 2 :])


def gather_in_order(shard, axes, turns):
    blocks = shard[None]
    for k in turns:
        blocks = lax.all_gather(blocks, axes[k], axis=0, tiled=True)
    block = [lax.axis_size(axes[k]) for k in reversed(turns)]
    blocks = blocks.reshape(*block, *shard.shape)
    turned = sorted(range(len(turns)), key=lambda place: turns[len(turns) - 1 - place])
    return blocks.transpose(*turned, *range(len(turns), blocks.ndim)).reshape(-1, *shard.shape)


def gather_axes(shard, axes, turns, dim):
    return joined_along(gather_in_order(shard, axes, turns), dim)


def split_up(shard, dim, length):
    before, after = (shard.shape[:dim], shard.shape[dim + 1 :])
    return jnp.moveaxis(shard.reshape(*before, length, -1, *after), dim, 0)


def sum_at_owner(shard, axis, dim):
    blocks = split_up(shard, dim, lax.axis_size(axis))
    arrived = lax.all_to_all(blocks, axis, split_axis=0, concat_axis=0, tiled=True)
    return arrived.sum(axis=0)


def from_everyone(shard, axis):
    length = lax.axis_size(axis)
    return lax.all_to_all(
        jnp.broadcast_to(shard[None], (length, *shard.shape)), axis, 0, 0, tiled=True
    )


def collect(shard, axis, dim):
    return joined_along(from_everyone(shard, axis), dim)


def matmul(left, right):
    return jnp.dot(left, right, precision=lax.Precision.HIGHEST, preferred_element_type=jnp.float32)


def matmul_left_t(left, right):
    return lax.dot_general(
        left,
        right,
        (((0,), (0,)), ((), ())),
        precision=lax.Precision.HIGHEST,
        preferred_element_type=jnp.float32,
    )


def select_rows(values, row_block, chosen):
    hit = jnp.any(row_block[:, None] == chosen[None, :], axis=1)
    return jnp.where(hit[:, None], values, jnp.float32(0.0))


def body(ancestor, panels, link_panels, diag_inverse, blocks):
    row_count = lax.axis_size(ROW)
    col_count = lax.axis_size("col")
    row_index = lax.axis_index(ROW)
    col_index = lax.axis_index("col")
    resident_t = ancestor.reshape(ancestor.shape[0] * ancestor.shape[1], ancestor.shape[2])
    supernodes = panels.shape[0]
    rows_here = panels.shape[1]
    panel_width = panels.shape[2]
    rows_part = panel_width // row_count
    cols_part = panel_width // col_count
    first_row = (row_index * col_count + col_index) * rows_here
    row_block = (first_row + jnp.arange(rows_here, dtype=jnp.int32)) // BLOCK
    masked = jnp.stack(
        [select_rows(panels[number], row_block, blocks[number]) for number in range(supernodes)]
    )
    joined = jnp.transpose(masked, (1, 0, 2)).reshape(rows_here, supernodes * panel_width)
    folded = matmul_left_t(resident_t, gather_axes(joined, ROW, (1, 0, 2), 0))
    summed = sum_at_owner(folded, "col", 0).reshape(rows_here, supernodes, panel_width)
    links_all = lax.all_gather(link_panels, ROW, axis=1, tiled=True)
    global_rows = row_index * rows_part + jnp.arange(rows_part, dtype=jnp.int32)
    lower_keep = jnp.arange(panel_width, dtype=jnp.int32)[None, :] <= global_rows[:, None]
    col_list = []
    diag_list = []
    prev_cols = None
    prev_rows = None
    for supernode in range(supernodes):
        local_panel = masked[supernode]
        product = summed[:, supernode, :]
        if supernode > 0:
            link = links_all[supernode - 1]
        lowered = jnp.where(lower_keep, diag_inverse[supernode], jnp.float32(0.0))
        right_part = lax.dynamic_slice_in_dim(lowered, col_index * cols_part, cols_part, 1)
        share = matmul(lowered.T, right_part)
        if supernode == 0:
            cols_now = -product
            partial_value = -matmul(local_panel.T, cols_now)
        else:
            carried = matmul(prev_cols, link)
            cols_now = -(product + carried)
            partial_value = matmul(carried.T, local_panel) - matmul(local_panel.T, cols_now)
            link_cols = lax.dynamic_slice_in_dim(link, col_index * cols_part, cols_part, 1)
            link_rows = lax.dynamic_slice_in_dim(link, row_index * rows_part, rows_part, 0)
            share = share + matmul(link_rows.T, matmul(prev_rows, link_cols))
        current = lax.dynamic_slice_in_dim(partial_value, col_index * cols_part, cols_part, 1)
        partial_value = lax.dynamic_update_slice_in_dim(
            partial_value, current + share, col_index * cols_part, 1
        )
        column_block = sum_at_owner(partial_value, "col", 1)
        diag_block = sum_at_owner(column_block, ROW, 0)
        if supernode + 1 < supernodes:
            prev_rows = collect(diag_block, "col", 1)
        col_list.append(cols_now)
        diag_list.append(diag_block)
        prev_cols = cols_now
    return (jnp.stack(col_list), jnp.stack(diag_list))


def solution(mesh):
    torus = Mesh(
        mesh.devices.reshape(8, 2, 2, mesh.shape["col"]), ("row_0", "row_1", "row_2", "col")
    )
    return jax.shard_map(
        body,
        mesh=torus,
        in_specs=(
            P(None, "col", ROW),
            P(None, ROW_COL, None),
            P(None, ROW, None),
            P(None, ROW, None),
            P(),
        ),
        out_specs=(P(None, ROW_COL, None), P(None, ROW, "col")),
        check_vma=False,
    )
```

profile of v0, /device:TPU:1, one launch (start us, length us, event | category | flops | bytes accessed | tf_op | source)
XLA Modules:
  0.0 295.9 jit_solution(991701370696724680)
XLA Ops:
  8.1 0.8 slice_bitcast_fusion
  8.9 0.2 compare_reduce_fusion.1
  9.1 0.9 slice_select_fusion
  10.0 0.1 copy.22
  10.1 0.1 broadcast_in_dim_reshape.3
  10.1 6.3 %all_gather.12 = f32[2,24,1024]{2,1,0:T(8,128)} all-gather(f32[1,24,1024]{2,1,0:T(8,128)S(1)} %broadcast_in_dim_reshape.3), channel_id=1, replica_groups=mesh['row_0'=8,'row_1'=2,'row_2'=2,'col'=16] {'row_1'}, dimensions={0}, use_global_device_ids=true | all-gather | bytes 294912 | tf_op jit(solution)/shard_map/all_gather | solution.py:21
  16.5 45.2 %all-gather.4.cloned.1.call-done = f32[16,24,1024]{2,1,0:T(8,128)} async-done(((f32[2,24,1024]{2,1,0:T(8,128)}), f32[16,24,1024]{2,1,0:T(8,128)}) %all-gather.4.cloned.1.call-update) | async-done | bytes 1572880 | tf_op jit(solution)/shard_map/all_gather | solution.py:21
  61.7 25.8 %all-gather.6.cloned.1.call-done = f32[32,24,1024]{2,1,0:T(8,128)} async-done(((f32[16,24,1024]{2,1,0:T(8,128)}), f32[32,24,1024]{2,1,0:T(8,128)}) %all-gather.6.cloned.1.call-update) | async-done | bytes 3145744 | tf_op jit(solution)/shard_map/all_gather | solution.py:21
  87.6 2.1 copy.23
  89.7 5.2 %fusion.35 = f32[1024,384]{0,1:T(8,128)} fusion(f32[768,1024]{1,0:T(8,128)S(1)} %bitcast.71, f32[768,384]{1,0:T(8,128)S(1)} %bitcast.70), kind=kOutput, calls=%fused_computation.58 | convolution fusion | flops 3623878656 | bytes 5898240 | tf_op jit(solution)/shard_map/dot_general | solution.py:59
  94.9 6.6 %all-to-all-start = ((f32[16,24,1024]{2,1,0:T(8,128)}), f32[16,24,1024]{2,1,0:T(8,128)S(1)}, u32[]{:S(2)}, u32[]{:S(2)}) async-start(f32[16,24,1024]{2,1,0:T(8,128)} %bitcast.72), calls=%async_computation | async-start | bytes 3145728 | tf_op jit(solution)/shard_map/all_to_all | solution.py:39
  101.5 0.5 all-gather.8.cloned.1.call-update
  102.2 35.6 %all-to-all-done = f32[16,24,1024]{2,1,0:T(8,128)S(1)} async-done(((f32[16,24,1024]{2,1,0:T(8,128)}), f32[16,24,1024]{2,1,0:T(8,128)S(1)}, u32[]{:S(2)}, u32[]{:S(2)}) %all-to-all-start) | async-done | bytes 1572896 | tf_op jit(solution)/shard_map/all_to_all | solution.py:39
  137.7 0.1 reduce_sum.45
  137.8 0.1 reshape.90
  138.0 2.0 convolution_negate_fusion
  140.0 1.8 fusion.2
  141.8 6.6 %all-to-all-start.1 = ((f32[16,512,32]{1,2,0:T(8,128)}), f32[16,512,32]{1,2,0:T(8,128)S(1)}, u32[]{:S(2)}, u32[]{:S(2)}) async-start(f32[16,512,32]{1,2,0:T(8,128)} %bitcast.17), calls=%async_computation.1 | async-start | bytes 2097152 | tf_op jit(solution)/shard_map/all_to_all | solution.py:39
  148.5 0.3 fusion.25
  148.8 50.5 %all-gather.8.cloned.1.call-done = f32[1,512,512]{2,1,0:T(8,128)} async-done(((f32[1,16,512]{2,1,0:T(8,128)}), f32[1,512,512]{2,1,0:T(8,128)}) %all-gather.8.cloned.1.call-update) | async-done | bytes 1048592 | tf_op jit(solution)/shard_map/all_gather | solution.py:92
  199.3 1.8 fusion.3
  201.3 0.1 copy.26
  201.4 0.8 reshape.96
  202.2 4.9 %all-to-all-start.2 = ((f32[32,1,512]{2,1,0:T(1,128)}), f32[32,1,512]{2,1,0:T(1,128)S(1)}, u32[]{:S(2)}, u32[]{:S(2)}) async-start(f32[32,1,512]{2,1,0:T(1,128)} %reshape.96), calls=%async_computation.2 | async-start | bytes 131072 | tf_op jit(solution)/shard_map/all_to_all | solution.py:39
  207.1 1.1 fusion.13
  208.2 8.7 %all-to-all-done.2 = f32[32,1,512]{2,1,0:T(1,128)S(1)} async-done(((f32[32,1,512]{2,1,0:T(1,128)}), f32[32,1,512]{2,1,0:T(1,128)S(1)}, u32[]{:S(2)}, u32[]{:S(2)}) %all-to-all-start.2) | async-done | bytes 65568 | tf_op jit(solution)/shard_map/all_to_all | solution.py:39
  216.9 0.5 broadcast.59
  217.4 0.8 reduce
  218.2 0.1 reshape.97
  218.4 0.7 reshape.98
  219.1 8.2 %all-to-all-start.3 = ((f32[16,1,512]{2,1,0:T(1,128)}), f32[16,1,512]{2,1,0:T(1,128)S(1)}, u32[]{:S(2)}, u32[]{:S(2)}) async-start(f32[16,1,512]{2,1,0:T(1,128)} %reshape.98), calls=%async_computation.3 | async-start | bytes 65536 | tf_op jit(solution)/shard_map/all_to_all | solution.py:45
  227.3 2.0 convolution_subtract_fusion
  229.3 5.7 %all-to-all-done.3 = f32[16,1,512]{2,1,0:T(1,128)S(1)} async-done(((f32[16,1,512]{2,1,0:T(1,128)}), f32[16,1,512]{2,1,0:T(1,128)S(1)}, u32[]{:S(2)}, u32[]{:S(2)}) %all-to-all-start.3) | async-done | bytes 32800 | tf_op jit(solution)/shard_map/all_to_all | solution.py:45
  235.0 0.7 reduce.1
  235.7 0.1 reshape.99
  235.9 0.1 reshape.93
  236.0 1.3 fusion.5
  237.3 1.7 fusion.1
  239.0 3.7 %all-to-all-start.4 = ((f32[16,512,32]{1,2,0:T(8,128)}), f32[16,512,32]{1,2,0:T(8,128)S(1)}, u32[]{:S(2)}, u32[]{:S(2)}) async-start(f32[16,512,32]{1,2,0:T(8,128)} %bitcast.26), calls=%async_computation.4 | async-start | bytes 2097152 | tf_op jit(solution)/shard_map/all_to_all | solution.py:39
  242.7 24.4 %all-to-all-done.4 = f32[16,512,32]{1,2,0:T(8,128)S(1)} async-done(((f32[16,512,32]{1,2,0:T(8,128)}), f32[16,512,32]{1,2,0:T(8,128)S(1)}, u32[]{:S(2)}, u32[]{:S(2)}) %all-to-all-start.4) | async-done | bytes 1048608 | tf_op jit(solution)/shard_map/all_to_all | solution.py:39
  267.2 0.1 copy.28
  267.3 0.8 reshape.100
  268.1 8.8 %all-to-all-start.5 = ((f32[32,1,512]{2,1,0:T(1,128)}), f32[32,1,512]{2,1,0:T(1,128)S(1)}, u32[]{:S(2)}, u32[]{:S(2)}) async-start(f32[32,1,512]{2,1,0:T(1,128)} %reshape.100), calls=%async_computation.5 | async-start | bytes 131072 | tf_op jit(solution)/shard_map/all_to_all | solution.py:39
  276.9 0.6 pad_maximum_fusion
  277.6 9.2 %all-to-all-done.5 = f32[32,1,512]{2,1,0:T(1,128)S(1)} async-done(((f32[32,1,512]{2,1,0:T(1,128)}), f32[32,1,512]{2,1,0:T(1,128)S(1)}, u32[]{:S(2)}, u32[]{:S(2)}) %all-to-all-start.5) | async-done | bytes 65568 | tf_op jit(solution)/shard_map/all_to_all | solution.py:39
  286.8 0.8 reduce.2
  287.6 0.1 reshape.101
  287.8 0.6 pad_maximum_fusion.1
  (25 shorter events, 0.7 us)
Async XLA Ops:
  8.0 81.7 %copy-start = (f32[32,24,384]{2,1,0:T(8,128)S(1)}, f32[32,24,384]{2,1,0:T(8,128)}, u32[]{:S(2)}) copy-start(f32[32,24,384]{2,1,0:T(8,128)} %param.5) | copy-start | bytes 3538948
  8.0 53.7 %all-gather.4.cloned.1.call-start = ((), (), s32[]{:S(2)}) async-start(), calls=%async_computation.6 | async-start | bytes 1769472 | tf_op jit(solution)/shard_map/all_gather | solution.py:21
  16.5 71.1 %all-gather.6.cloned.1.call-start = ((), (), s32[]{:S(2)}) async-start(), calls=%async_computation.7 | async-start | bytes 4718592 | tf_op jit(solution)/shard_map/all_gather | solution.py:21
  94.9 7.2 %copy-start.2 = (f32[2,16,512]{2,1,0:T(8,128)S(1)}, f32[2,16,512]{2,1,0:T(8,128)}, u32[]{:S(2)}) copy-start(f32[2,16,512]{2,1,0:T(8,128)} %param.8) | copy-start | bytes 196612
  94.9 42.9 %all-to-all-start = ((f32[16,24,1024]{2,1,0:T(8,128)}), f32[16,24,1024]{2,1,0:T(8,128)S(1)}, u32[]{:S(2)}, u32[]{:S(2)}) async-start(f32[16,24,1024]{2,1,0:T(8,128)} %bitcast.72), calls=%async_computation | async-start | bytes 3145728 | tf_op jit(solution)/shard_map/all_to_all | solution.py:39
  101.5 97.8 %all-gather.8.cloned.1.call-start = ((), (), s32[]{:S(2)}) async-start(), calls=%async_computation.8 | async-start | bytes 1081344 | tf_op jit(solution)/shard_map/all_gather | solution.py:92
  141.8 59.4 %all-to-all-start.1 = ((f32[16,512,32]{1,2,0:T(8,128)}), f32[16,512,32]{1,2,0:T(8,128)S(1)}, u32[]{:S(2)}, u32[]{:S(2)}) async-start(f32[16,512,32]{1,2,0:T(8,128)} %bitcast.17), calls=%async_computation.1 | async-start | bytes 2097152 | tf_op jit(solution)/shard_map/all_to_all | solution.py:39
  148.5 58.6 %copy-start.1 = (f32[2,24,512]{2,1,0:T(8,128)S(1)}, f32[2,24,512]{2,1,0:T(8,128)}, u32[]{:S(2)}) copy-start(f32[2,24,512]{2,1,0:T(8,128)} %param.6) | copy-start | bytes 294916
  202.2 14.7 %all-to-all-start.2 = ((f32[32,1,512]{2,1,0:T(1,128)}), f32[32,1,512]{2,1,0:T(1,128)S(1)}, u32[]{:S(2)}, u32[]{:S(2)}) async-start(f32[32,1,512]{2,1,0:T(1,128)} %reshape.96), calls=%async_computation.2 | async-start | bytes 131072 | tf_op jit(solution)/shard_map/all_to_all | solution.py:39
  219.1 15.9 %all-to-all-start.3 = ((f32[16,1,512]{2,1,0:T(1,128)}), f32[16,1,512]{2,1,0:T(1,128)S(1)}, u32[]{:S(2)}, u32[]{:S(2)}) async-start(f32[16,1,512]{2,1,0:T(1,128)} %reshape.98), calls=%async_computation.3 | async-start | bytes 65536 | tf_op jit(solution)/shard_map/all_to_all | solution.py:45
  239.0 28.1 %all-to-all-start.4 = ((f32[16,512,32]{1,2,0:T(8,128)}), f32[16,512,32]{1,2,0:T(8,128)S(1)}, u32[]{:S(2)}, u32[]{:S(2)}) async-start(f32[16,512,32]{1,2,0:T(8,128)} %bitcast.26), calls=%async_computation.4 | async-start | bytes 2097152 | tf_op jit(solution)/shard_map/all_to_all | solution.py:39
  268.1 18.7 %all-to-all-start.5 = ((f32[32,1,512]{2,1,0:T(1,128)}), f32[32,1,512]{2,1,0:T(1,128)S(1)}, u32[]{:S(2)}, u32[]{:S(2)}) async-start(f32[32,1,512]{2,1,0:T(1,128)} %reshape.100), calls=%async_computation.5 | async-start | bytes 131072 | tf_op jit(solution)/shard_map/all_to_all | solution.py:39
Sparse Core Ops, SparseCore 0:
  16.6 45.0 all-gather.3
  63.8 23.6 all-gather.5
Sparse Core Ops, SparseCore 1:
  105.3 93.9 all-gather.7
where the time goes:
time: 297 us; the launch traced here: 296 us
  waiting for transfers between devices  206 us (69%)
  starting transfers between devices  38.9 us (13%)
  matrix products  17.3 us (6%)
  between operations  15.8 us (5%)
  local copies, waits for them, and re-layouts  6.79 us (2%)
  blocking collectives  6.33 us (2%)
  other arithmetic  5.08 us (2%)
    all_to_all x5, waiting for transfers between devices, sum_at_owner(): lax.all_to_all(blocks, axis, split_axis=0, concat_axis=0, tiled=True)  77.9 us
    all_gather x2, waiting for transfers between devices, gather_in_order(): blocks = lax.all_gather(blocks, axes[k], axis=0, tiled=True)  71 us
    all_gather x1, waiting for transfers between devices, body(): links_all = lax.all_gather(link_panels, ROW, axis=1, tiled=True)  50.5 us
    all_to_all x5, starting transfers between devices, sum_at_owner(): lax.all_to_all(blocks, axis, split_axis=0, concat_axis=0, tiled=True)  30.6 us
    dot_general x8, matrix products, matmul(): jnp.dot(left, right, precision=lax.Precision.HIGHEST, preferred_element_t...  12.1 us
    all_to_all x1, starting transfers between devices, from_everyone(): lax.all_to_all(jnp.broadcast_to(shard[None], (length, *shard.shape)), axi...  8.19 us
    all_gather x1, blocking collectives, gather_in_order(): blocks = lax.all_gather(blocks, axes[k], axis=0, tiled=True)  6.33 us
  transfers between devices with their start and end apart: 9, of which 8 were waited for; matrix products, arithmetic and copies ran while one was open for 3% of the time, Pallas kernels for 0%

commit v1 on v0

v1 whole, which is shorter than its diff:
```python
import jax
import jax.numpy as jnp
from jax import lax
from jax.experimental import pallas as pl
from jax.experimental.pallas import tpu as pltpu
from jax.sharding import PartitionSpec as P

BLOCK = 128
F32 = jnp.float32
BF16 = jnp.bfloat16
MESH = pl.DeviceIdType.MESH


def halves_of(value):
    high = value.astype(BF16)
    return high, (value - high.astype(F32)).astype(BF16)


def dot(left, right):
    return jnp.dot(left, right, preferred_element_type=F32)


def dot3(lh, ll, rh, rl):
    return dot(lh, rh) + (dot(lh, rl) + dot(ll, rh))


def kernel(
    pay, anc, low, cols, diag,
    pbuf, ebuf, ehi, elo, fbuf, xa, sap, sam, rap, ram, sbp, sbm, rbp, rbm, xbs, xb,
    bhi, blo, prh, prl, ssend, sbuf, dsend, dbuf, tsend, tbuf, gsend, gbuf,
    esem, ag_s, ag_r, rs_s, rs_r, ex_s, ex_r,
):
    r = lax.axis_index("row")
    c = lax.axis_index("col")
    z, xh, k = r // 4, (r // 2) % 2, r % 2
    y, xl = c // 2, c % 2
    kk = r // 2

    def at_row(zz, hh, co):
        return (lax.rem(zz + 8, 8) * 4 + hh * 2 + co, c)

    def at_col(yy, ll):
        return (r, lax.rem(yy + 8, 8) * 2 + ll)

    zp, zm = at_row(z + 1, xh, k), at_row(z - 1, xh, k)
    xpart, cpart = at_row(z, 1 - xh, k), at_row(z, xh, 1 - k)
    yp, ym, lpart = at_col(y + 1, xl), at_col(y - 1, xl), at_col(y, 1 - xl)

    fetch = pltpu.make_async_copy(anc, ebuf, esem)
    fetch.start()

    barrier = pltpu.get_barrier_semaphore()
    near = (zp, zm, xpart, cpart, yp, ym, lpart)
    for peer in near:
        pl.semaphore_signal(barrier, inc=1, device_id=peer, device_id_type=MESH)
    pl.semaphore_wait(barrier, len(near))

    sends = []

    def remote(src, dst, ss, rs, to):
        return pltpu.make_async_remote_copy(
            src_ref=src, dst_ref=dst, send_sem=ss, recv_sem=rs, device_id=to, device_id_type=MESH
        )

    def chip(zz, hh):
        return lax.rem(zz + 8, 8) * 2 + hh

    ring = {}

    def ag(name, src, block, to):
        n = len(ring)
        ring[name] = remote(src, pbuf.at[block, k], ag_s.at[n], ag_r.at[n], to)
        ring[name].start()
        sends.append(ring[name])

    def arrived(name, block):
        ring[name].wait_recv()
        return pbuf.at[block, k]

    mine = chip(z, xh)
    other = chip(z, 1 - xh)
    ag("x", pay, mine, xpart)
    ag("po0", pay, mine, zp)
    ag("mo0", pay, mine, zm)
    ag("cx", pay, mine, cpart)
    pbuf[mine, k] = pay[...]

    fetch.wait()
    for i in range(6):
        h, l = halves_of(ebuf[i * 128 : (i + 1) * 128, :].T)
        ehi[:, i * 128 : (i + 1) * 128] = h
        elo[:, i * 128 : (i + 1) * 128] = l

    src = arrived("x", other)
    ag("pp0", src, other, zp)
    ag("mp0", src, other, zm)
    ag("cp", src, other, cpart)
    for s in range(4):
        for tag, sign, hh, last in (("po", -1, xh, 3), ("mo", 1, xh, 2), ("pp", -1, 1 - xh, 2), ("mp", 1, 1 - xh, 3)):
            if s > last:
                continue
            block = chip(z + sign * (s + 1), hh)
            src = arrived(f"{tag}{s}", block)
            if s < last:
                ag(f"{tag}{s + 1}", src, block, zp if sign < 0 else zm)
            ag(f"c{tag}{s}", src, block, cpart)
    for name in list(ring):
        if name[0] == "c":
            ring[name].wait_recv()

    rsn = []

    def rs(src, dst, to):
        n = len(rsn)
        copy = remote(src, dst, rs_s.at[n], rs_r.at[n], to)
        rsn.append(copy)
        sends.append(copy)
        copy.start()
        return copy

    def product(half):
        def step(n, _):
            at = pl.ds(pl.multiple_of(half * 512 + n * 256, 256), 256)
            ph, plo = halves_of(pbuf[:, :, 0:24, at].reshape(768, 256))
            fbuf[:, :, :, at] = dot3(ehi[...], elo[...], ph, plo).reshape(8, 2, 24, 256)
            return 0

        lax.fori_loop(0, 2, step, 0)

    def yy(d):
        return lax.rem(y + d + 8, 8)

    A, B = pl.ds(0, 512), pl.ds(512, 512)
    product(0)
    xac = {}
    for d in (4, 3, -3, 2, -2, 1, -1, 0):
        xac[d] = rs(fbuf.at[yy(d), 1 - xl, :, A], xa.at[yy(d)], lpart)
    product(1)
    bp = [rs(fbuf.at[yy(3), :, :, B], rbp.at[0], yp)]
    bm = [rs(fbuf.at[yy(-4), :, :, B], rbm.at[0], ym)]

    for g in range(4):
        part = pbuf[g * 4 : g * 4 + 4, :, 24:32, :].reshape(8, 8, 1024)
        rows = jnp.concatenate([part[:, :, 0:512], part[:, :, 512:1024]], axis=1).reshape(128, 512)
        h, l = halves_of(rows)
        bhi[g * 128 : (g + 1) * 128, :] = h
        blo[g * 128 : (g + 1) * 128, :] = l
    for g in range(2):
        h, l = halves_of(pbuf[g * 8 : g * 8 + 8, pl.ds(k, 1), 0:24, :].reshape(192, 1024))
        rows = slice(g * 192, (g + 1) * 192)
        prh[rows, 0:1024] = h
        prl[rows, 0:1024] = l
        rh, rl = halves_of(dot3(h[:, 0:512], l[:, 0:512], bhi[...], blo[...]))
        prh[rows, 1024:1536] = rh
        prl[rows, 1024:1536] = rl
    lane = lax.broadcasted_iota(jnp.int32, (1, 128), 1)
    l0 = low[0]
    l1 = low[1]
    h, l = halves_of(l0)
    m0 = dot3(h, l, bhi[...], blo[...])
    gsend[0:16, 0:512] = l0
    gsend[16:32, 0:512] = l1
    gsend[32:48, 0:512] = m0
    chunk = gsend[0:48, pl.ds(pl.multiple_of((c // 4) * 128, 128), 128)]
    off = lax.rem(c, 4) * 32
    to0 = pltpu.roll(chunk, lax.rem(128 - off, 128), 1)
    to1 = pltpu.roll(chunk, lax.rem(160 - off, 128), 1)
    row = lax.broadcasted_iota(jnp.int32, (48, 128), 0)
    wide = jnp.where(row < 16, jnp.where(lane < 32, to0, 0.0), jnp.where((lane >= 32) & (lane < 64), to1, 0.0))
    wide = wide + pltpu.roll(wide, 64, 1)
    ut = jnp.concatenate([gsend[0:48, 0:512], jnp.zeros((80, 512), F32)], axis=0).T
    wide = jnp.concatenate([wide, jnp.zeros((80, 128), F32)], axis=0)
    uh, ul = halves_of(ut)
    wh, wl = halves_of(wide)
    gpart = dot3(uh, ul, wh, wl).reshape(32, 2, 8, 128)
    gbuf[0] = jnp.where(lane < 64, gpart[:, 0], gpart[:, 1])

    def send_g(i, _):
        to = lax.rem(r + i, 32)
        remote(gbuf.at[0, to], gbuf.at[1, r], ex_s.at[0], ex_r.at[0], (to, c)).start()
        return 0

    lax.fori_loop(1, 32, send_g, 0)
    gbuf[1, r] = gbuf[0, r]

    xac[4].wait_recv()
    sap[0] = fbuf[yy(4), xl, :, A] + xa[yy(4)]
    ap = [rs(sap.at[0], rap.at[0], yp)]
    am = []
    for s in range(1, 4):
        if s < 3:
            bp[s - 1].wait_recv()
            sbp[s] = fbuf[yy(3 - s), :, :, B] + rbp[s - 1]
            bp.append(rs(sbp.at[s], rbp.at[s], yp))
        bm[s - 1].wait_recv()
        sbm[s] = fbuf[yy(s - 4), :, :, B] + rbm[s - 1]
        bm.append(rs(sbm.at[s], rbm.at[s], ym))
        xac[4 - s].wait_recv()
        ap[s - 1].wait_recv()
        sap[s] = fbuf[yy(4 - s), xl, :, A] + xa[yy(4 - s)] + rap[s - 1]
        ap.append(rs(sap.at[s], rap.at[s], yp))
        xac[s - 4].wait_recv()
        if s == 1:
            sam[0] = fbuf[yy(-3), xl, :, A] + xa[yy(-3)]
        else:
            am[s - 2].wait_recv()
            sam[s - 1] = fbuf[yy(s - 4), xl, :, A] + xa[yy(s - 4)] + ram[s - 2]
        am.append(rs(sam.at[s - 1], ram.at[s - 1], ym))
    bp[2].wait_recv()
    bm[3].wait_recv()
    xbs[...] = fbuf[y, :, :, B] + rbp[2] + rbm[3]
    xbc = rs(xbs.at[1 - xl], xb, lpart)
    xac[0].wait_recv()
    ap[3].wait_recv()
    am[2].wait_recv()
    c0 = -(fbuf[y, xl, :, A] + xa[y] + rap[3] + ram[2])
    h, l = halves_of(c0)
    carried = dot3(h, l, bhi[...], blo[...])
    xbc.wait_recv()
    c1 = -(xbs[xl] + xb[...] + carried)
    cols[0] = c0
    cols[1] = c1

    for q in range(16):
        at = slice((q // 4) * 128, (q // 4) * 128 + 128)
        o = (q % 4) * 32

        def turned(value, place):
            shift = (place - o) % 128
            return value if shift == 0 else pltpu.roll(value, shift, 1)

        ssend[q] = jnp.where(
            lane < 32,
            turned(c0[:, at], 0),
            jnp.where(lane < 64, turned(c1[:, at], 32), jnp.where(lane < 96, turned(carried[:, at], 64), 0.0)),
        )

    def send_s(i, _):
        to = lax.rem(kk + i, 16)
        remote(ssend.at[to], sbuf.at[kk], ex_s.at[1], ex_r.at[1], (to * 2 + k, c)).start()
        return 0

    lax.fori_loop(1, 16, send_s, 0)
    sbuf[kk] = ssend[kk]

    def settle(buf, count, sem):
        pltpu.make_async_copy(buf.at[pl.ds(0, count)], buf.at[pl.ds(0, count)], sem).wait()

    settle(sbuf, 15, ex_r.at[1])
    h, l = halves_of(sbuf[...].reshape(384, 128).T)
    out = dot3(h, l, prh[...], prl[...])
    d0 = -out[0:32, 0:512]
    d1 = -(out[32:64, 512:1024] + out[64:96, 1024:1536])
    dt = jnp.concatenate([d0, d1, d0, d1], axis=0).T.reshape(32, 2, 8, 128)
    dsend[...] = jnp.where(lane < 64, dt[:, 0], dt[:, 1])
    tt = out[64:96, 512:1024].reshape(2, 2, 8, 512)
    for q in range(16):
        at = slice((q // 4) * 128, (q // 4) * 128 + 128)
        o = (q % 4) * 32
        for half in range(2):
            first, second = tt[half, 0, :, at], tt[half, 1, :, at]
            s1, s2 = (32 - o) % 128, (96 - o) % 128
            first = first if s1 == 0 else pltpu.roll(first, s1, 1)
            second = second if s2 == 0 else pltpu.roll(second, s2, 1)
            tsend[q * 2 + half] = jnp.where(
                lane >= 96, second, jnp.where((lane >= 32) & (lane < 64), first, 0.0)
            )
    slot = c * 2 + k

    def send_d(i, _):
        to = lax.rem(r + i, 32)
        remote(dsend.at[to], dbuf.at[slot], ex_s.at[2], ex_r.at[2], (to, kk)).start()
        return 0

    def send_t(i, _):
        to = lax.rem(slot + i, 32)
        remote(tsend.at[to], tbuf.at[slot], ex_s.at[3], ex_r.at[3], (kk * 2 + lax.rem(to, 2), to // 2)).start()
        return 0

    lax.fori_loop(1, 32, send_d, 0)
    inside = kk == c

    @pl.when(inside)
    def _():
        dbuf[slot] = dsend[r]

    @pl.when(jnp.logical_not(inside))
    def _():
        remote(dsend.at[r], dbuf.at[slot], ex_s.at[4], ex_r.at[2], (r, kk)).start()

    lax.fori_loop(1, 32, send_t, 0)
    tbuf[slot] = tsend[slot]

    settle(gbuf.at[1], 31, ex_r.at[0])
    total = jnp.sum(gbuf[1], axis=0)
    settle(tbuf, 31, ex_r.at[3])
    total = total + jnp.sum(tbuf[...], axis=0)

    @pl.when(inside)
    def _():
        settle(dbuf, 31, ex_r.at[2])

    @pl.when(jnp.logical_not(inside))
    def _():
        settle(dbuf, 32, ex_r.at[2])
        settle(dsend, 1, ex_s.at[4])

    total = total + jnp.sum(dbuf[...], axis=0)
    diag[0, 0:8, :] = total[:, 0:32]
    diag[1, 0:8, :] = pltpu.roll(total, 96, 1)[:, 0:32]
    diag[0, 8:16, :] = pltpu.roll(total, 64, 1)[:, 0:32]
    diag[1, 8:16, :] = pltpu.roll(total, 32, 1)[:, 0:32]

    settle(gbuf.at[1], 31, ex_s.at[0])
    settle(sbuf, 15, ex_s.at[1])
    settle(dbuf, 31, ex_s.at[2])
    settle(tbuf, 31, ex_s.at[3])
    for copy in sends:
        copy.wait_send()


def body(ancestor, panels, link_panels, diag_inverse, blocks):
    r = lax.axis_index("row")
    c = lax.axis_index("col")
    resident = ancestor.reshape(768, 384)
    first = (r * 16 + c) * 24
    row_block = (first + jnp.arange(24, dtype=jnp.int32)) // BLOCK
    hit = jnp.any(row_block[None, :, None] == blocks[:, None, :], axis=2)
    masked = jnp.where(hit[:, :, None], panels, jnp.float32(0.0))
    link = link_panels[0]
    pay = jnp.concatenate(
        [
            jnp.concatenate([masked[0], masked[1]], axis=1),
            jnp.concatenate([link[0:8], link[8:16]], axis=1),
        ],
        axis=0,
    )
    rows = r * 16 + jnp.arange(16, dtype=jnp.int32)
    keep = jnp.arange(512, dtype=jnp.int32)[None, :] <= rows[:, None]
    low = jnp.where(keep[None], diag_inverse, jnp.float32(0.0))
    vmem = pl.BlockSpec(memory_space=pltpu.VMEM)
    return pl.pallas_call(
        kernel,
        out_shape=(
            jax.ShapeDtypeStruct((2, 24, 512), F32),
            jax.ShapeDtypeStruct((2, 16, 32), F32),
        ),
        in_specs=[vmem, pl.BlockSpec(memory_space=pl.ANY), vmem],
        out_specs=(vmem, vmem),
        scratch_shapes=[
            pltpu.VMEM((16, 2, 32, 1024), F32),
            pltpu.VMEM((768, 384), F32),
            pltpu.VMEM((384, 768), BF16),
            pltpu.VMEM((384, 768), BF16),
            pltpu.VMEM((8, 2, 24, 1024), F32),
            pltpu.VMEM((8, 24, 512), F32),
            pltpu.VMEM((4, 24, 512), F32),
            pltpu.VMEM((3, 24, 512), F32),
            pltpu.VMEM((4, 24, 512), F32),
            pltpu.VMEM((3, 24, 512), F32),
            pltpu.VMEM((3, 2, 24, 512), F32),
            pltpu.VMEM((4, 2, 24, 512), F32),
            pltpu.VMEM((3, 2, 24, 512), F32),
            pltpu.VMEM((4, 2, 24, 512), F32),
            pltpu.VMEM((2, 24, 512), F32),
            pltpu.VMEM((24, 512), F32),
            pltpu.VMEM((512, 512), BF16),
            pltpu.VMEM((512, 512), BF16),
            pltpu.VMEM((384, 1536), BF16),
            pltpu.VMEM((384, 1536), BF16),
            pltpu.VMEM((16, 24, 128), F32),
            pltpu.VMEM((16, 24, 128), F32),
            pltpu.VMEM((32, 8, 128), F32),
            pltpu.VMEM((32, 8, 128), F32),
            pltpu.VMEM((32, 8, 128), F32),
            pltpu.VMEM((32, 8, 128), F32),
            pltpu.VMEM((48, 512), F32),
            pltpu.VMEM((2, 32, 8, 128), F32),
            pltpu.SemaphoreType.DMA,
            pltpu.SemaphoreType.DMA((31,)),
            pltpu.SemaphoreType.DMA((31,)),
            pltpu.SemaphoreType.DMA((23,)),
            pltpu.SemaphoreType.DMA((23,)),
            pltpu.SemaphoreType.DMA((5,)),
            pltpu.SemaphoreType.DMA((4,)),
        ],
        compiler_params=pltpu.CompilerParams(
            collective_id=0, has_side_effects=True, vmem_limit_bytes=40 * 1024 * 1024
        ),
    )(pay, resident, low)


def solution(mesh):
    return jax.shard_map(
        body,
        mesh=mesh,
        in_specs=(
            P(None, "col", "row"),
            P(None, ("row", "col"), None),
            P(None, "row", None),
            P(None, "row", None),
            P(),
        ),
        out_specs=(P(None, ("row", "col"), None), P(None, "row", "col")),
        check_vma=False,
    )
```

time: 297 us -> 93.8 us (0.32)
  waiting for transfers between devices: 206 us -> 0 us
  Pallas kernels: 0 us -> 85.8 us
  starting transfers between devices: 38.9 us -> 0 us
  matrix products: 17.3 us -> 0 us
  between operations: 15.8 us -> 0.67 us
  blocking collectives: 6.33 us -> 0 us
  local copies, waits for them, and re-layouts: 6.79 us -> 3.27 us
    all_gather x3 -> x0, waiting for transfers between devices: 122 us -> none  [the longest x2 71 us: gather_in_order(): blocks = lax.all_gather(blocks, axes[k], axis=0, tiled=True)]
    pallas_call x0 -> x1, Pallas kernels: none -> 85.8 us  [body(): pl.pallas_call(kernel, out_shape=(jax.ShapeDtypeStruct((2, 24, 512), F32)...]
    all_to_all x6 -> x0, waiting for transfers between devices: 83.6 us -> none  [the longest x5 77.9 us: sum_at_owner(): lax.all_to_all(blocks, axis, split_axis=0, concat_axis=0, tiled=True)]
    all_to_all x6 -> x0, starting transfers between devices: 38.8 us -> none  [the longest x5 30.6 us: sum_at_owner(): lax.all_to_all(blocks, axis, split_axis=0, concat_axis=0, tiled=True)]
    dot_general x9 -> x0, matrix products: 17.3 us -> none  [the longest x8 12.1 us: matmul(): jnp.dot(left, right, precision=lax.Precision.HIGHEST, preferred_element_t...]
    all_gather x1 -> x0, blocking collectives: 6.33 us -> none  [gather_in_order(): blocks = lax.all_gather(blocks, axes[k], axis=0, tiled=True)]
  transfers between devices with their start and end apart: 9 -> 0, of which waited for: 8 -> 0; matrix products, arithmetic and copies ran while one was open for 3% -> 0% of each run, Pallas kernels for 0% -> 0%
where the time goes in v1:
time: 93.8 us; the launch traced here: 92.5 us
  Pallas kernels  85.8 us (91%)
  local copies, waits for them, and re-layouts  3.27 us (3%)
  other arithmetic  2.78 us (3%)
    pallas_call x1, Pallas kernels, body(): pl.pallas_call(kernel, out_shape=(jax.ShapeDtypeStruct((2, 24, 512), F32)...  85.8 us
    unnamed x4, local copies, waits for them, and re-layouts  2.52 us

profile of v1, /device:TPU:1, one launch (start us, length us, event | category | flops | bytes accessed | tf_op | source)
XLA Modules:
  0.0 92.5 jit_solution(14197453131503242382)
XLA Ops:
  0.7 0.9 compare_reduce_fusion
  1.5 1.0 %broadcast_select_fusion = f32[2,24,512]{2,1,0:T(8,128)S(1)} fusion(f32[2,24,512]{2,1,0:T(8,128)} %param.6, pred[2,24]{1,0:T(4,128)(4,1)S(1)} %compare_reduce_fusion), kind=kLoop, calls=%fused_computation.3 | loop fusion | flops 24576 | bytes 196656 | tf_op jit(solution)/shard_map/jit(_where)/select_n | solution.py:329
  2.5 0.7 slice_bitcast_fusion.3
  3.3 0.1 iota_compare_fusion
  3.3 0.8 broadcast_select_fusion.1.low
  4.2 0.0 copy-start
  4.2 1.3 %copy-done = f32[32,24,384]{2,1,0:T(8,128)S(1)} copy-done((f32[32,24,384]{2,1,0:T(8,128)S(1)}, f32[32,24,384]{2,1,0:T(8,128)}, u32[]{:S(2)}) %copy-start) | copy-done | bytes 1179672
  5.5 85.8 %shard_map.68 = (f32[2,24,512]{2,1,0:T(8,128)S(1)}, f32[2,16,32]{2,1,0:T(8,128)S(1)}) custom-call(f32[32,1024]{1,0:T(8,128)S(1)} %maximum_maximum_fusion.pay, f32[768,384]{1,0:T(8,128)S(1)} %bitcast.9, f32[2,16,512]{2,1,0:T(8,128)S(1)} %broadcast_select_fusion.1.low), custom_call_target="tpu_custom_call" | custom-call | tf_op jit(solution)/shard_map/pallas_call | solution.py:342
  91.2 0.6 copy.9
  91.9 0.6 copy.10
  (4 shorter events, 0.0 us)
Async XLA Ops:
  4.2 1.3 %copy-start = (f32[32,24,384]{2,1,0:T(8,128)S(1)}, f32[32,24,384]{2,1,0:T(8,128)}, u32[]{:S(2)}) copy-start(f32[32,24,384]{2,1,0:T(8,128)} %param.5) | copy-start | bytes 3538948

commit v2 on v0

v2 whole, which is shorter than its diff:
```python
import jax
import jax.numpy as jnp
from jax import lax
from jax.experimental import pallas as pl
from jax.experimental.pallas import tpu as pltpu
from jax.sharding import PartitionSpec as P

BLOCK = 128
F32 = jnp.float32
BF16 = jnp.bfloat16
MESH = pl.DeviceIdType.MESH


def halves_of(value):
    high = value.astype(BF16)
    return high, (value - high.astype(F32)).astype(BF16)


def dot(left, right):
    return jnp.dot(left, right, preferred_element_type=F32)


def dot3(lh, ll, rh, rl):
    return dot(lh, rh) + (dot(lh, rl) + dot(ll, rh))


def turned(value, shift):
    shift = shift % 128
    return value if shift == 0 else pltpu.roll(value, shift, 1)


def kernel(
    anc, pan, lnk, inv, blk, cols, diag,
    pb0, pb1, bb, praw, low, hits, ebuf, ehi, elo, f0, f1, xa, sbuf, rbuf,
    bhi, blo, prh, prl, s0send, s0buf, s1send, s1buf, dsend, dbuf, tsend, tbuf, gsend, gbuf,
    in_s, ag_s, ag_r, rs_s, rs_r, ex_s, ex_r,
):
    r = lax.axis_index("row")
    c = lax.axis_index("col")
    z, xh, k = r // 4, (r // 2) % 2, r % 2
    y, xl = c // 2, c % 2
    kk = r // 2
    lane = lax.broadcasted_iota(jnp.int32, (1, 128), 1)

    def wrap(i):
        return lax.rem(i + 8, 8)

    def at_row(zz, hh, co):
        return (wrap(zz) * 4 + hh * 2 + co, c)

    def at_col(yy, ll):
        return (r, wrap(yy) * 2 + ll)

    xpart, cpart = at_row(z, 1 - xh, k), at_row(z, xh, 1 - k)
    lpart = at_col(y, 1 - xl)

    barrier = pltpu.get_barrier_semaphore()
    near = [xpart, cpart, lpart]
    for d in (2, -2, 1, -1):
        near += [at_row(z + d, xh, k), at_col(y + d, xl)]
    for peer in near:
        pl.semaphore_signal(barrier, inc=1, device_id=peer, device_id_type=MESH)

    fetches = [
        pltpu.make_async_copy(src, dst, in_s.at[n])
        for n, (src, dst) in enumerate(
            ((pan, praw), (blk, hits), (anc, ebuf), (lnk.at[0], bb.at[kk, k]), (inv, low))
        )
    ]
    for fetch in fetches:
        fetch.start()

    first = (r * 16 + c) * 24
    b0 = first // BLOCK
    b1 = (first + 23) // BLOCK
    fetches[0].wait()
    fetches[1].wait()
    upper = lax.broadcasted_iota(jnp.int32, (24, 512), 0) < (b0 + 1) * BLOCK - first
    for s, pb in enumerate((pb0, pb1)):
        row = hits[s : s + 1, :]
        hit0 = jnp.max(jnp.where(row == b0, 1.0, 0.0), axis=1, keepdims=True)
        hit1 = jnp.max(jnp.where(row == b1, 1.0, 0.0), axis=1, keepdims=True)
        keep = jnp.where(upper, hit0, hit1)
        pb[kk, k] = jnp.where(keep > 0.5, praw[s], 0.0)

    pl.semaphore_wait(barrier, len(near))

    sends = []

    def remote(src, dst, ss, rs, to):
        return pltpu.make_async_remote_copy(
            src_ref=src, dst_ref=dst, send_sem=ss, recv_sem=rs, device_id=to, device_id_type=MESH
        )

    streams = (pb0, pb1, bb)
    place = (kk, z * 2 + 1 - xh)
    far = (1, -1)
    ring = {}

    def ag(q, name, block, to):
        n = len(ring)
        ref = streams[q].at[block, k]
        copy = remote(ref, ref, ag_s.at[n], ag_r.at[n], to)
        ring[q, name] = copy
        sends.append(copy)
        copy.start()

    def across(q):
        ag(q, "x", kk, xpart)

    def crossed(q):
        ring[q, "x"].wait_recv()

    def level1(q, line):
        for d in (2, -2, 1, -1):
            ag(q, f"{line}{d}", place[line], at_row(z + d, xh, k))
        ag(q, f"c{line}", place[line], cpart)

    def block_from(d, line):
        return wrap(z - d) * 2 + (xh if line == 0 else 1 - xh)

    def level2(q, line):
        for g in (far[line], -far[line]):
            ring[q, f"{line}{2 * g}"].wait_recv()
            block = block_from(2 * g, line)
            if g == far[line]:
                ag(q, f"{line}{4 * g}", block, at_row(z + 2 * g, xh, k))
            ag(q, f"{line}{3 * g}", block, at_row(z + g, xh, k))
            ag(q, f"c{line}{2 * g}", block, cpart)

    def handed(q, line, distances):
        for d in distances:
            ring[q, f"{line}{d}"].wait_recv()
            ag(q, f"c{line}{d}", block_from(d, line), cpart)

    def ones(q):
        handed(q, 0, (1, -1))
        handed(q, 1, (1, -1))

    def lasts(q, line):
        handed(q, line, (3 * far[line], -3 * far[line], 4 * far[line]))

    def close_stream(q):
        for (stream, name), copy in list(ring.items()):
            if stream == q and name[0] == "c":
                copy.wait_recv()

    rsn = []

    def rs(src, dst, to):
        n = len(rsn)
        copy = remote(src, dst, rs_s.at[n], rs_r.at[n], to)
        rsn.append(copy)
        sends.append(copy)
        copy.start()
        return copy

    def product(pb, out):
        def step(n, _):
            at = pl.ds(pl.multiple_of(n * 256, 256), 256)
            ph, plo = halves_of(pb[:, :, :, at].reshape(768, 256))
            out[:, :, :, at] = dot3(ehi[...], elo[...], ph, plo).reshape(8, 2, 24, 256)
            return 0

        lax.fori_loop(0, 2, step, 0)

    def yy(d):
        return wrap(y + d)

    folded = (f0, f1)
    tree = {}

    def exchange(s):
        g = far[s]
        for d in (4 * g, 3 * g, -3 * g, 2 * g, -2 * g, g, -g, 0):
            tree[s, "x", d] = rs(folded[s].at[yy(d), 1 - xl], xa.at[s, yy(d)], lpart)

    def value(s, d):
        tree[s, "x", d].wait_recv()
        return folded[s][yy(d), xl] + xa[s, yy(d)]

    def arrive(s, d):
        tree[s, d].wait_recv()
        return rbuf[s, slots.index(d * far[s])]

    slots = [4, 3, -3, 2, -2, 1, -1]

    def pass_on(s, d, part, to):
        n = slots.index(d * far[s])
        sbuf[s, n] = part
        tree[s, d] = rs(sbuf.at[s, n], rbuf.at[s, n], at_col(y + to, xl))

    def sum_a(s):
        g = far[s]
        pass_on(s, 4 * g, value(s, 4 * g), 2 * g)
        pass_on(s, 3 * g, value(s, 3 * g), g)
        pass_on(s, -3 * g, value(s, -3 * g), -g)

    def sum_b(s):
        g = far[s]
        part = value(s, 2 * g) + arrive(s, 3 * g)
        pass_on(s, 2 * g, part + arrive(s, 4 * g), 2 * g)
        pass_on(s, -2 * g, value(s, -2 * g) + arrive(s, -3 * g), -2 * g)

    def sum_c(s):
        g = far[s]
        pass_on(s, g, value(s, g), g)
        pass_on(s, -g, value(s, -g), -g)

    def summed(s):
        total = value(s, 0)
        for d in (1, -1, -2, 2):
            total = total + arrive(s, d * far[s])
        return total

    across(0)
    level1(0, 0)
    across(1)
    fetches[3].wait()
    across(2)
    fetches[2].wait()
    for i in range(6):
        at = slice(i * 128, (i + 1) * 128)
        h, l = halves_of(ebuf[at, :].T)
        ehi[:, at] = h
        elo[:, at] = l
    crossed(0)
    level1(0, 1)
    level2(0, 0)
    level2(0, 1)
    level1(1, 0)
    crossed(1)
    level1(1, 1)
    ones(0)
    lasts(0, 0)
    lasts(0, 1)
    close_stream(0)
    product(pb0, f0)
    exchange(0)
    level2(1, 0)
    level2(1, 1)
    crossed(2)
    level1(2, 0)
    level1(2, 1)
    sum_a(0)
    ones(1)
    lasts(1, 0)
    lasts(1, 1)
    close_stream(1)
    product(pb1, f1)
    exchange(1)
    sum_b(0)
    level2(2, 0)
    level2(2, 1)
    sum_c(0)
    for g in range(3):
        at = slice(g * 128, (g + 1) * 128)
        rows = slice(g * 8, g * 8 + 8)
        for s, pb in enumerate((pb0, pb1)):
            h, l = halves_of(pb[:, pl.ds(k, 1), rows, :].reshape(128, 512))
            prh[at, s * 512 : s * 512 + 512] = h
            prl[at, s * 512 : s * 512 + 512] = l
    sum_a(1)
    ones(2)
    lasts(2, 0)
    lasts(2, 1)
    sum_b(1)
    sum_c(1)
    close_stream(2)
    for g in range(4):
        at = slice(g * 128, (g + 1) * 128)
        h, l = halves_of(bb[g * 4 : g * 4 + 4].reshape(128, 512))
        bhi[at, :] = h
        blo[at, :] = l

    c0 = -summed(0)
    h, l = halves_of(c0)
    carried = dot3(h, l, bhi[...], blo[...])
    cols[0] = c0

    def owner(chip):
        zc, hc = chip // 2, chip % 2
        return lax.rem(16 - zc - y, 8) * 2 + jnp.where(hc == xl, 0, 1)

    def packed(value, q):
        at = slice((q // 4) * 128, (q // 4) * 128 + 128)
        o = (q % 4) * 32
        v = [turned(value[g * 8 : g * 8 + 8, at], g * 32 - o) for g in range(3)]
        return jnp.where(lane < 32, v[0], jnp.where(lane < 64, v[1], v[2]))

    part = owner(kk)

    def settle(buf, count, sem):
        pltpu.make_async_copy(buf.at[pl.ds(0, count)], buf.at[pl.ds(0, count)], sem).wait()

    def spread(send, recv, n):
        def step(i, _):
            to = lax.rem(kk + i, 16)
            remote(send.at[owner(to)], recv.at[kk], ex_s.at[n], ex_r.at[n], (to * 2 + k, c)).start()
            return 0

        lax.fori_loop(1, 16, step, 0)
        recv[kk] = send[part]

    for q in range(16):
        s0send[q, 0] = packed(c0, q)
        s0send[q, 1] = packed(carried, q)
    spread(s0send, s0buf, 1)

    for g in range(3):
        at = slice(g * 128, (g + 1) * 128)
        rh, rl = halves_of(dot3(prh[at, 0:512], prl[at, 0:512], bhi[...], blo[...]))
        prh[at, 1024:1536] = rh
        prl[at, 1024:1536] = rl

    c1 = -(summed(1) + carried)
    for q in range(16):
        s1send[q] = packed(c1, q)
    spread(s1send, s1buf, 2)
    cols[1] = c1

    fetches[4].wait()
    tri = lax.broadcasted_iota(jnp.int32, (16, 512), 1) <= r * 16 + lax.broadcasted_iota(jnp.int32, (16, 512), 0)
    l0 = jnp.where(tri, low[0], 0.0)
    l1 = jnp.where(tri, low[1], 0.0)
    h, l = halves_of(l0)
    gsend[0:16, :] = l0
    gsend[16:32, :] = l1
    gsend[32:48, :] = dot3(h, l, bhi[...], blo[...])
    chunk = gsend[:, pl.ds(pl.multiple_of((c // 4) * 128, 128), 128)]
    off = lax.rem(c, 4) * 32
    to0 = pltpu.roll(chunk, lax.rem(128 - off, 128), 1)
    to1 = pltpu.roll(chunk, lax.rem(160 - off, 128), 1)
    row = lax.broadcasted_iota(jnp.int32, (48, 128), 0)
    wide = jnp.where(row < 16, jnp.where(lane < 32, to0, 0.0), jnp.where((lane >= 32) & (lane < 64), to1, 0.0))
    wide = wide + pltpu.roll(wide, 64, 1)
    zeros = jnp.zeros((80, 512), F32)
    uh, ul = halves_of(jnp.concatenate([gsend[...], zeros], axis=0).T)
    wh, wl = halves_of(jnp.concatenate([wide, zeros[:, 0:128]], axis=0))
    gpart = dot3(uh, ul, wh, wl).reshape(32, 2, 8, 128)
    gbuf[0] = jnp.where(lane < 64, gpart[:, 0], gpart[:, 1])

    def send_g(i, _):
        to = lax.rem(r + i, 32)
        remote(gbuf.at[0, to], gbuf.at[1, r], ex_s.at[0], ex_r.at[0], (to, c)).start()
        return 0

    lax.fori_loop(1, 32, send_g, 0)
    gbuf[1, r] = gbuf[0, r]

    def left_of(tiles):
        t = tiles.reshape(128, 128).T
        return jnp.concatenate([t[0:32], t[32:64], t[64:96]], axis=1)

    slot = c * 2 + k

    def scatter(send, recv, n, start, target, inside):
        def step(i, _):
            to = lax.rem(start + i, 32)
            remote(send.at[to], recv.at[slot], ex_s.at[n], ex_r.at[n], target(to)).start()
            return 0

        lax.fori_loop(1, 32, step, 0)

        @pl.when(inside)
        def _():
            recv[slot] = send[start]

        @pl.when(jnp.logical_not(inside))
        def _():
            remote(send.at[start], recv.at[slot], ex_s.at[n], ex_r.at[n], target(start)).start()

    def settle_scatter(buf, sem, inside):
        @pl.when(inside)
        def _():
            settle(buf, 31, sem)

        @pl.when(jnp.logical_not(inside))
        def _():
            settle(buf, 32, sem)

    settle(s0buf, 15, ex_r.at[1])
    h, l = halves_of(jnp.concatenate([left_of(s0buf[:, 0]), left_of(s0buf[:, 1])], axis=0))
    out = dot3(h, l, prh[...], prl[...])
    d0 = -out[0:32, 0:512]
    kept = out[32:64, 1024:1536]
    tt = out[32:64, 512:1024].reshape(2, 2, 8, 512)
    for q in range(16):
        at = slice((q // 4) * 128, (q // 4) * 128 + 128)
        o = (q % 4) * 32
        for half in range(2):
            upper_rows = turned(tt[half, 0, :, at], 32 - o)
            lower_rows = turned(tt[half, 1, :, at], 96 - o)
            tsend[q * 2 + half] = jnp.where(
                lane >= 96, lower_rows, jnp.where((lane >= 32) & (lane < 64), upper_rows, 0.0)
            )
    t_inside = part == kk
    scatter(tsend, tbuf, 3, slot, lambda to: (part * 2 + lax.rem(to, 2), to // 2), t_inside)

    settle(s1buf, 15, ex_r.at[2])
    h, l = halves_of(left_of(s1buf[...]))
    d1 = -(dot3(h, l, prh[:, 512:1024], prl[:, 512:1024]) + kept)
    dt = jnp.concatenate([d0, d1, d0, d1], axis=0).T.reshape(32, 2, 8, 128)
    dsend[...] = jnp.where(lane < 64, dt[:, 0], dt[:, 1])
    d_inside = part == c
    scatter(dsend, dbuf, 4, r, lambda to: (to, part), d_inside)

    settle(gbuf.at[1], 31, ex_r.at[0])
    total = jnp.sum(gbuf[1], axis=0)
    settle_scatter(tbuf, ex_r.at[3], t_inside)
    total = total + jnp.sum(tbuf[...], axis=0)
    settle_scatter(dbuf, ex_r.at[4], d_inside)
    total = total + jnp.sum(dbuf[...], axis=0)
    diag[0, 0:8, :] = total[:, 0:32]
    diag[1, 0:8, :] = turned(total, 96)[:, 0:32]
    diag[0, 8:16, :] = turned(total, 64)[:, 0:32]
    diag[1, 8:16, :] = turned(total, 32)[:, 0:32]

    settle(gbuf.at[1], 31, ex_s.at[0])
    settle(s0buf, 15, ex_s.at[1])
    settle(s1buf, 15, ex_s.at[2])
    settle_scatter(tbuf, ex_s.at[3], t_inside)
    settle_scatter(dbuf, ex_s.at[4], d_inside)
    for copy in sends:
        copy.wait_send()


def body(ancestor, panels, link_panels, diag_inverse, blocks):
    vmem = pl.BlockSpec(memory_space=pltpu.VMEM)
    there = pl.BlockSpec(memory_space=pl.ANY)
    dma = pltpu.SemaphoreType.DMA
    return pl.pallas_call(
        kernel,
        out_shape=(
            jax.ShapeDtypeStruct((2, 24, 512), F32),
            jax.ShapeDtypeStruct((2, 16, 32), F32),
        ),
        in_specs=[there] * 5,
        out_specs=(vmem, vmem),
        scratch_shapes=[
            pltpu.VMEM((16, 2, 24, 512), F32),
            pltpu.VMEM((16, 2, 24, 512), F32),
            pltpu.VMEM((16, 2, 16, 512), F32),
            pltpu.VMEM((2, 24, 512), F32),
            pltpu.VMEM((2, 16, 512), F32),
            pltpu.VMEM((2, 48), jnp.int32),
            pltpu.VMEM((768, 384), F32),
            pltpu.VMEM((384, 768), BF16),
            pltpu.VMEM((384, 768), BF16),
            pltpu.VMEM((8, 2, 24, 512), F32),
            pltpu.VMEM((8, 2, 24, 512), F32),
            pltpu.VMEM((2, 8, 24, 512), F32),
            pltpu.VMEM((2, 7, 24, 512), F32),
            pltpu.VMEM((2, 7, 24, 512), F32),
            pltpu.VMEM((512, 512), BF16),
            pltpu.VMEM((512, 512), BF16),
            pltpu.VMEM((384, 1536), BF16),
            pltpu.VMEM((384, 1536), BF16),
            pltpu.VMEM((16, 2, 8, 128), F32),
            pltpu.VMEM((16, 2, 8, 128), F32),
            pltpu.VMEM((16, 8, 128), F32),
            pltpu.VMEM((16, 8, 128), F32),
            pltpu.VMEM((32, 8, 128), F32),
            pltpu.VMEM((32, 8, 128), F32),
            pltpu.VMEM((32, 8, 128), F32),
            pltpu.VMEM((32, 8, 128), F32),
            pltpu.VMEM((48, 512), F32),
            pltpu.VMEM((2, 32, 8, 128), F32),
            dma((5,)),
            dma((93,)),
            dma((93,)),
            dma((30,)),
            dma((30,)),
            dma((5,)),
            dma((5,)),
        ],
        compiler_params=pltpu.CompilerParams(
            collective_id=0, has_side_effects=True
        ),
    )(
        ancestor.reshape(ancestor.shape[0] * ancestor.shape[1], ancestor.shape[2]),
        panels,
        link_panels,
        diag_inverse,
        blocks,
    )


def solution(mesh):
    return jax.shard_map(
        body,
        mesh=mesh,
        in_specs=(
            P(None, "col", "row"),
            P(None, ("row", "col"), None),
            P(None, "row", None),
            P(None, "row", None),
            P(),
        ),
        out_specs=(P(None, ("row", "col"), None), P(None, "row", "col")),
        check_vma=False,
    )
```

time: 297 us -> 79.1 us (0.27)
  waiting for transfers between devices: 206 us -> 0 us
  Pallas kernels: 0 us -> 75.3 us
  starting transfers between devices: 38.9 us -> 0 us
  matrix products: 17.3 us -> 0 us
  between operations: 15.8 us -> 0.64 us
  blocking collectives: 6.33 us -> 0 us
  other arithmetic: 5.08 us -> 0 us
  local copies, waits for them, and re-layouts: 6.79 us -> 2.86 us
    all_gather x3 -> x0, waiting for transfers between devices: 122 us -> none  [the longest x2 71 us: gather_in_order(): blocks = lax.all_gather(blocks, axes[k], axis=0, tiled=True)]
    all_to_all x6 -> x0, waiting for transfers between devices: 83.6 us -> none  [the longest x5 77.9 us: sum_at_owner(): lax.all_to_all(blocks, axis, split_axis=0, concat_axis=0, tiled=True)]
    pallas_call x0 -> x1, Pallas kernels: none -> 75.3 us  [body(): pl.pallas_call(kernel, out_shape=(jax.ShapeDtypeStruct((2, 24, 512), F32)...]
    all_to_all x6 -> x0, starting transfers between devices: 38.8 us -> none  [the longest x5 30.6 us: sum_at_owner(): lax.all_to_all(blocks, axis, split_axis=0, concat_axis=0, tiled=True)]
    dot_general x9 -> x0, matrix products: 17.3 us -> none  [the longest x8 12.1 us: matmul(): jnp.dot(left, right, precision=lax.Precision.HIGHEST, preferred_element_t...]
    all_gather x1 -> x0, blocking collectives: 6.33 us -> none  [gather_in_order(): blocks = lax.all_gather(blocks, axes[k], axis=0, tiled=True)]
  transfers between devices with their start and end apart: 9 -> 0, of which waited for: 8 -> 0; matrix products, arithmetic and copies ran while one was open for 3% -> 0% of each run, Pallas kernels for 0% -> 0%
where the time goes in v2:
time: 79.1 us; the launch traced here: 78.8 us
  Pallas kernels  75.3 us (95%)
  local copies, waits for them, and re-layouts  2.86 us (4%)
    pallas_call x1, Pallas kernels, body(): pl.pallas_call(kernel, out_shape=(jax.ShapeDtypeStruct((2, 24, 512), F32)...  75.3 us
    unnamed x2, local copies, waits for them, and re-layouts  2.86 us

profile of v2, /device:TPU:1, one launch (start us, length us, event | category | flops | bytes accessed | tf_op | source)
XLA Modules:
  0.0 78.8 jit_solution(13137584865857127088)
XLA Ops:
  0.6 75.3 %shard_map.68 = (f32[2,24,512]{2,1,0:T(8,128)}, f32[2,16,32]{2,1,0:T(8,128)}) custom-call(f32[768,384]{1,0:T(8,128)} %bitcast.1, f32[2,24,512]{2,1,0:T(8,128)} %pan.1, f32[1,16,512]{2,1,0:T(8,128)} %lnk.1, f32[2,16,512]{2,1,0:T(8,128)} %inv.1, s32[2,48]{1,0:T(2,128)} %blk.1), custom_call_target="tpu_custom_call" | custom-call | tf_op jit(solution)/shard_map/pallas_call | solution.py:432
  76.0 1.5 %copy.9 = f32[2,24,512]{2,1,0:T(8,128)} copy(f32[2,24,512]{2,1,0:T(8,128)} %get-tuple-element.4) | data formatting | bytes 196608
  77.5 1.3 %copy.10 = f32[2,16,32]{2,1,0:T(8,128)} copy(f32[2,16,32]{2,1,0:T(8,128)} %get-tuple-element.5) | data formatting | bytes 8192

commit v3 on v2

--- a/solution.py
+++ b/solution.py
@@ -22,6 +22,12 @@
 
 def dot3(lh, ll, rh, rl):
     return dot(lh, rh) + (dot(lh, rl) + dot(ll, rh))
+
+
+def thin(lh, ll, rh, rl):
+    rows = lh.shape[0]
+    both = dot(jnp.concatenate([lh, ll], axis=0), rh)
+    return both[0:rows] + (both[rows:] + dot(lh, rl))
 
 
 def turned(value, shift):
@@ -253,6 +259,7 @@
     level2(2, 0)
     level2(2, 1)
     sum_c(0)
+    sum_a(1)
     for g in range(3):
         at = slice(g * 128, (g + 1) * 128)
         rows = slice(g * 8, g * 8 + 8)
@@ -260,7 +267,6 @@
             h, l = halves_of(pb[:, pl.ds(k, 1), rows, :].reshape(128, 512))
             prh[at, s * 512 : s * 512 + 512] = h
             prl[at, s * 512 : s * 512 + 512] = l
-    sum_a(1)
     ones(2)
     lasts(2, 0)
     lasts(2, 1)
@@ -307,12 +313,6 @@
         s0send[q, 1] = packed(carried, q)
     spread(s0send, s0buf, 1)
 
-    for g in range(3):
-        at = slice(g * 128, (g + 1) * 128)
-        rh, rl = halves_of(dot3(prh[at, 0:512], prl[at, 0:512], bhi[...], blo[...]))
-        prh[at, 1024:1536] = rh
-        prl[at, 1024:1536] = rl
-
     c1 = -(summed(1) + carried)
     for q in range(16):
         s1send[q] = packed(c1, q)
@@ -326,7 +326,7 @@
     h, l = halves_of(l0)
     gsend[0:16, :] = l0
     gsend[16:32, :] = l1
-    gsend[32:48, :] = dot3(h, l, bhi[...], blo[...])
+    gsend[32:48, :] = thin(h, l, bhi[...], blo[...])
     chunk = gsend[:, pl.ds(pl.multiple_of((c // 4) * 128, 128), 128)]
     off = lax.rem(c, 4) * 32
     to0 = pltpu.roll(chunk, lax.rem(128 - off, 128), 1)
@@ -348,6 +348,12 @@
     lax.fori_loop(1, 32, send_g, 0)
     gbuf[1, r] = gbuf[0, r]
 
+    for g in range(3):
+        at = slice(g * 128, (g + 1) * 128)
+        rh, rl = halves_of(dot3(prh[at, 0:512], prl[at, 0:512], bhi[...], blo[...]))
+        prh[at, 1024:1536] = rh
+        prl[at, 1024:1536] = rl
+
     def left_of(tiles):
         t = tiles.reshape(128, 128).T
         return jnp.concatenate([t[0:32], t[32:64], t[64:96]], axis=1)
@@ -381,7 +387,7 @@
 
     settle(s0buf, 15, ex_r.at[1])
     h, l = halves_of(jnp.concatenate([left_of(s0buf[:, 0]), left_of(s0buf[:, 1])], axis=0))
-    out = dot3(h, l, prh[...], prl[...])
+    out = thin(h, l, prh[...], prl[...])
     d0 = -out[0:32, 0:512]
     kept = out[32:64, 1024:1536]
     tt = out[32:64, 512:1024].reshape(2, 2, 8, 512)
@@ -399,7 +405,7 @@
 
     settle(s1buf, 15, ex_r.at[2])
     h, l = halves_of(left_of(s1buf[...]))
-    d1 = -(dot3(h, l, prh[:, 512:1024], prl[:, 512:1024]) + kept)
+    d1 = -(thin(h, l, prh[:, 512:1024], prl[:, 512:1024]) + kept)
     dt = jnp.concatenate([d0, d1, d0, d1], axis=0).T.reshape(32, 2, 8, 128)
     dsend[...] = jnp.where(lane < 64, dt[:, 0], dt[:, 1])
     d_inside = part == c
@@ -475,14 +481,19 @@
             dma((5,)),
         ],
         compiler_params=pltpu.CompilerParams(
-            collective_id=0, has_side_effects=True
+            collective_id=0, has_side_effects=True, vmem_limit_bytes=56300000
         ),
     )(
-        ancestor.reshape(ancestor.shape[0] * ancestor.shape[1], ancestor.shape[2]),
-        panels,
-        link_panels,
-        diag_inverse,
-        blocks,
+        *(
+            pltpu.with_memory_space_constraint(value, pltpu.HBM)
+            for value in (
+                ancestor.reshape(ancestor.shape[0] * ancestor.shape[1], ancestor.shape[2]),
+                panels,
+                link_panels,
+                diag_inverse,
+                blocks,
+            )
+        )
     )
 
 

time: 79.1 us -> 76.8 us (0.971)
  local copies, waits for them, and re-layouts: 2.86 us -> 1.25 us
    unnamed x2, local copies, waits for them, and re-layouts: 2.86 us -> 1.25 us
where the time goes in v3:
time: 76.8 us; the launch traced here: 76.7 us
  Pallas kernels  74.8 us (97%)
  local copies, waits for them, and re-layouts  1.25 us (2%)
    pallas_call x1, Pallas kernels, body(): pl.pallas_call(kernel, out_shape=(jax.ShapeDtypeStruct((2, 24, 512), F32)...  74.8 us

profile of v3, /device:TPU:1, one launch (start us, length us, event | category | flops | bytes accessed | tf_op | source)
XLA Modules:
  0.0 76.7 jit_solution(9596435707277925670)
XLA Ops:
  0.6 74.8 %shard_map.68 = (f32[2,24,512]{2,1,0:T(8,128)S(1)}, f32[2,16,32]{2,1,0:T(8,128)S(1)}) custom-call(f32[768,384]{1,0:T(8,128)} %bitcast.1, f32[2,24,512]{2,1,0:T(8,128)} %pan.1, f32[1,16,512]{2,1,0:T(8,128)} %lnk.1, f32[2,16,512]{2,1,0:T(8,128)} %inv.1, s32[2,48]{1,0:T(2,128)} %blk.1), custom_call_target="tpu_custom_call" | custom-call | tf_op jit(solution)/shard_map/pallas_call | solution.py:438
  75.5 0.6 copy.9
  76.1 0.6 copy.10
